TPU v7x, 256 devices: a whole 4x4x8 slice. The times are simulated.
256 devices in a mesh: row: 16 (over x, y), col: 8 (over z), depth: 2 (over core).
Axes of the slice: x: 4, y: 4, z: 8, core: 2. Of those that a mesh axis runs over, the one named last changes fastest.
Arguments:
- halves: bfloat16 [2, 8192, 16384], P(None, 'row', ('col', 'depth')), may hold values from -6 to 6
- spectrum: float32 [2, 16384], P(None, ('col', 'depth')), as said below
- wanted: int32 [4096], P('col'), may hold values from 0 to 32766, as said below
- fraction: float32 [4096], P('col'), may hold values from 0.05 to 0.95
Outputs:
- eigvec: float32 [2, 8192, 4096], P(None, 'row', ('col', 'depth'))
Inputs may be any that keep to these rules, and one draw needn't show every extreme that they name: Read in the order spectrum[0,0], spectrum[1,0], spectrum[0,1], spectrum[1,1], ... the values rise strictly, each by more than 0.05 over the one before. `wanted`: distinct positions in that merged order of the 32768 eigenvalues.
All inputs are finite; a program needn't handle non-finite values.
Results may differ from a plain program's by a relative error of at most 0.0029.
Values may be sent and summed in bfloat16 or wider, within the bound.
No kernel may reach another device: no remote copies, remote signals or barrier semaphores. Data moves between devices by JAX's collectives and lax.ppermute only.
A program may use at most 128 MiB of HBM per device.

v0:
```python
import functools
import math
import jax
import jax.numpy as jnp
from jax import lax
from jax.sharding import Mesh
from jax.sharding import PartitionSpec as P

ROW = ("row_0", "row_1")


def over_axes(shard, axes):
    return functools.reduce(lax.psum, axes, shard)


def in_one_piece(arrays, axis, dim, along):
    both = jnp.concatenate(arrays, axis=along)
    out, at, done = (lax.all_gather(both, axis, axis=dim, tiled=True), 0, [])
    for a in arrays:
        done.append(lax.slice_in_dim(out, at, at + a.shape[along], axis=along))
        at += a.shape[along]
    return tuple(done)


def cut_along(shard, dim, size):
    shape = shard.shape
    pieces = shard.reshape(*shape[:dim], size, shape[dim] // size, *shape[dim + 1 :])
    return jnp.moveaxis(pieces, dim, 0)


def summed_on_arrival(shard, axis, dim):
    pieces = cut_along(shard, dim, lax.axis_size(axis))
    arrived = lax.all_to_all(pieces, axis, split_axis=0, concat_axis=0, tiled=True)
    return arrived.sum(axis=0)


def root_terms(spectrum_full, wanted):
    ordered = jnp.stack([spectrum_full[0], spectrum_full[1]], axis=1).reshape(-1)
    lower = jnp.take(ordered, wanted)
    upper = jnp.take(ordered, wanted + 1)
    return (lower, upper - lower)


def cauchy_block(seam_part, value_part, lower, width, frac):
    return seam_part[:, :, None] / (
        value_part[:, :, None] - lower[None, None, :] - frac[None, None, :] * width[None, None, :]
    )


def column_norms(seam_full, value_full, lower, width, frac):
    step = seam_full.shape[1] // 8
    total = jnp.zeros(lower.shape, jnp.float32)
    for part in range(8):
        cauchy = cauchy_block(
            seam_full[:, part * step : (part + 1) * step],
            value_full[:, part * step : (part + 1) * step],
            lower,
            width,
            frac,
        )
        total = total + jnp.sum(cauchy * cauchy, axis=(0, 1))
    return jnp.sqrt(total)


def panel_product(piece, seam_part, value_part, lower, width, frac):
    columns = lower.shape[0]
    block = math.gcd(columns, 128)

    def one(index):
        start = index * block
        low = lax.dynamic_slice_in_dim(lower, start, block)
        wid = lax.dynamic_slice_in_dim(width, start, block)
        frc = lax.dynamic_slice_in_dim(frac, start, block)
        cauchy = cauchy_block(seam_part, value_part, low, wid, frc)
        product = jnp.einsum(
            "arh,ahk->ark", piece, cauchy.astype(jnp.bfloat16), preferred_element_type=jnp.float32
        )
        return (product, jnp.zeros((block,), jnp.float32))

    products, sums = lax.map(one, jnp.arange(columns // block))
    product = jnp.transpose(products, (1, 2, 0, 3)).reshape(piece.shape[0], piece.shape[1], columns)
    return (product, sums.reshape(-1))


def body(halves, spectrum, wanted, fraction):
    rows_here = halves.shape[1]
    shard_width = halves.shape[2]
    place = lax.axis_index(ROW)
    low_row = jnp.where(
        place == lax.axis_size(ROW) - 1, halves[0, rows_here - 1].astype(jnp.float32), 0.0
    )
    high_row = jnp.where(place == 0, halves[1, 0].astype(jnp.float32), 0.0)
    seam = over_axes(jnp.stack([low_row, high_row]), ROW)
    seam_full, value_full = in_one_piece((seam, spectrum), ("col", "depth"), 1, 0)
    lower_col, width_col = root_terms(value_full, wanted)
    ncols = lax.axis_size("col")
    ndepth = lax.axis_size("depth")
    layer = lax.axis_index("depth")
    seam_mine = lax.dynamic_index_in_dim(
        seam_full.reshape(2, ncols, ndepth, shard_width), layer, 2, keepdims=False
    ).reshape(2, ncols * shard_width)
    value_mine = lax.dynamic_index_in_dim(
        value_full.reshape(2, ncols, ndepth, shard_width), layer, 2, keepdims=False
    ).reshape(2, ncols * shard_width)
    share = lower_col.shape[0] // ndepth
    product, sums = panel_product(
        lax.all_gather(halves, "col", axis=2, tiled=True),
        seam_mine,
        value_mine,
        lower_col,
        width_col,
        fraction,
    )
    total = product
    product = summed_on_arrival(total, "depth", 2)
    lower_own = lax.dynamic_slice_in_dim(lower_col, layer * share, share)
    width_own = lax.dynamic_slice_in_dim(width_col, layer * share, share)
    frac_own = lax.dynamic_slice_in_dim(fraction, layer * share, share)
    norms = column_norms(seam_full, value_full, lower_own, width_own, frac_own)
    return product / norms[None, None, :]


def solution(mesh):
    split = Mesh(
        mesh.devices.reshape(4, 4, mesh.shape["col"], mesh.shape["depth"]),
        ("row_0", "row_1", "col", "depth"),
    )
    in_specs = (P(None, ROW, ("col", "depth")), P(None, ("col", "depth")), P("col"), P("col"))
    out_specs = P(None, ROW, ("col", "depth"))
    return jax.shard_map(body, mesh=split, in_specs=in_specs, out_specs=out_specs, check_vma=False)
```

profile of v0, /device:TPU:1, one launch (start us, length us, event | category | flops | bytes accessed | tf_op | source)
XLA Modules:
  0.0 244.6 jit_solution(11194111778540224851)
XLA Ops:
  6.5 0.7 all-gather.2.cloned.1.call-update
  7.3 0.7 fusion.7
  8.1 9.4 %psum.14 = f32[2,1024]{1,0:T(2,128)S(1)} all-reduce(f32[2,1024]{1,0:T(2,128)S(1)} %pad_maximum_fusion.2), channel_id=1, replica_groups=mesh['row_0'=4,'row_1'=4,'col'=8,'depth'=2] {'row_0'}, use_global_device_ids=true, to_apply=%region_0.1 | all-reduce | flops 2048 | bytes 16384 | tf_op jit(solution)/shard_map/psum | solution.py:13
  17.5 9.0 %psum.15 = f32[2,1024]{1,0:T(2,128)S(1)} all-reduce(f32[2,1024]{1,0:T(2,128)S(1)} %psum.14), channel_id=1, replica_groups=mesh['row_0'=4,'row_1'=4,'col'=8,'depth'=2] {'row_1'}, use_global_device_ids=true, to_apply=%region_1.2 | all-reduce | flops 2048 | bytes 16384 | tf_op jit(solution)/shard_map/psum | solution.py:13
  26.5 0.7 pad_maximum_fusion.1
  27.2 26.9 %all_gather.6 = f32[4,16384]{1,0:T(4,128)S(1)} all-gather(f32[4,1024]{1,0:T(4,128)S(1)} %pad_maximum_fusion.1), channel_id=1, replica_groups=mesh['row_0'=4,'row_1'=4,'col'=8,'depth'=2] {'col','depth'}, dimensions={1}, use_global_device_ids=true | all-gather | bytes 278528 | tf_op jit(solution)/shard_map/all_gather | solution.py:18
  54.4 5.0 %copy.20 = f32[16384,2]{1,0:T(8,128)} copy(f32[16384,2]{0,1:T(2,128)S(1)} %pad_maximum_fusion) | data formatting | bytes 262144 | tf_op jit(solution)/shard_map/stack | solution.py:38
  59.3 7.0 %reshape.100 = f32[32768]{0:T(1024)S(1)} reshape(f32[16384,2]{1,0:T(8,128)} %copy.20) | data formatting | bytes 262144 | tf_op jit(solution)/shard_map/reshape | solution.py:38
  66.4 3.1 %gather_fusion = f32[512]{0:T(512)S(1)} fusion(f32[32768]{0:T(1024)S(1)} %reshape.100, s32[1024]{0:T(1024)S(1)} %get-tuple-element.109), kind=kCustom, calls=%fused_computation.clone | custom fusion | bytes 6144 | tf_op jit(solution)/shard_map/jit(_take)/gather | solution.py:39
  69.5 3.1 %gather_fusion.1 = f32[512]{0:T(512)S(1)} fusion(f32[32768]{0:T(1024)S(1)} %reshape.100, s32[1024]{0:T(1024)S(1)} %get-tuple-element.108), kind=kCustom, calls=%fused_computation.1.clone | custom fusion | bytes 6144 | tf_op jit(solution)/shard_map/jit(_take)/gather | solution.py:40
  73.6 9.4 %multiply_reduce_fusion.6 = (f32[256]{0:T(256)S(1)}, f32[256]{0:T(256)S(1)}, f32[256]{0:T(256)S(1)}, f32[256]{0:T(256)S(1)}, f32[256]{0:T(256)S(1)}, /*index=5*/f32[256]{0:T(256)S(1)}, f32[256]{0:T(256)S(1)}, f32[256]{0:T(256)S(1)}) fusion(f32[2,2048]{1,0:T(2,128)S(1)} %get-tuple-element.97, f32[2,2048]{1,0:T(2,128)S(1)} %get-tuple-element.98, ...), kind=kLoop, calls=%fused_computation.17 | loop fusion | flops 41940992 | bytes 272384 | tf_op jit(solution)/shard_map/reduce_sum | solution.py:61
  83.0 0.6 add_sqrt_fusion
  83.6 103.3 %all-gather.2.cloned.1.call-done = bf16[2,512,8192]{2,1,0:T(8,128)(2,1)} async-done(((bf16[2,512,1024]{2,1,0:T(8,128)(2,1)}), bf16[2,512,8192]{2,1,0:T(8,128)(2,1)}) %all-gather.2.cloned.1.call-update) | async-done | bytes 16777232 | tf_op jit(solution)/shard_map/all_gather | solution.py:107
  186.9 43.0 %while.10 = (s32[]{:T(128)}, f32[4,2,512,128]{2,3,0,1:T(8,128)S(1)}, f32[2,8,1024]{2,1,0:T(8,128)S(1)}, f32[2,8,1024]{2,1,0:T(8,128)S(1)}, s32[4]{0:T(128)S(1)},...) while((s32[]{:T(128)}, ...), condition=%wide.region_3.5_spmd, body=%wide.region_2.4_spmd.sunk | while | flops 2155872512 | bytes 17698500 | solution.py:80
  186.9 0.6 dynamic_slice.46
  188.3 9.3 %fusion.15 = f32[4,2,512,128]{2,3,0,1:T(8,128)S(1)} fusion(f32[4,2,512,128]{2,3,0,1:T(8,128)S(1)} %get-tuple-element.179, s32[]{:T(128)} %get-tuple-element.178, bf16[2,512,8192]{2,1,0:T(8,128)(2,1)} %get-tuple-element.199, f32[128]{0:T(128)S(1)} %dynamic-slice_multiply_fusion.3, f32[128]{0:T(128)S(1)} %dynamic_slice.47, f32[2,8192]{1,0:T(2,128)S(1)} %bitcast.52, ...), kind=kOutput, calls=%fused_computation.9.clone.1 | convolution fusion | flops 2155872256 | bytes 17433604 | tf_op jit(solution)/shard_map/while/body/eval_jaxpr/arh,ahk->ark/dot_general | solution.py:75
  197.7 0.6 dynamic_slice.46
  199.1 9.3 %fusion.15 = f32[4,2,512,128]{2,3,0,1:T(8,128)S(1)} fusion(f32[4,2,512,128]{2,3,0,1:T(8,128)S(1)} %get-tuple-element.179, s32[]{:T(128)} %get-tuple-element.178, bf16[2,512,8192]{2,1,0:T(8,128)(2,1)} %get-tuple-element.199, f32[128]{0:T(128)S(1)} %dynamic-slice_multiply_fusion.3, f32[128]{0:T(128)S(1)} %dynamic_slice.47, f32[2,8192]{1,0:T(2,128)S(1)} %bitcast.52, ...), kind=kOutput, calls=%fused_computation.9.clone.1 | convolution fusion | flops 2155872256 | bytes 17433604 | tf_op jit(solution)/shard_map/while/body/eval_jaxpr/arh,ahk->ark/dot_general | solution.py:75
  208.4 0.6 dynamic_slice.46
  209.8 9.3 %fusion.15 = f32[4,2,512,128]{2,3,0,1:T(8,128)S(1)} fusion(f32[4,2,512,128]{2,3,0,1:T(8,128)S(1)} %get-tuple-element.179, s32[]{:T(128)} %get-tuple-element.178, bf16[2,512,8192]{2,1,0:T(8,128)(2,1)} %get-tuple-element.199, f32[128]{0:T(128)S(1)} %dynamic-slice_multiply_fusion.3, f32[128]{0:T(128)S(1)} %dynamic_slice.47, f32[2,8192]{1,0:T(2,128)S(1)} %bitcast.52, ...), kind=kOutput, calls=%fused_computation.9.clone.1 | convolution fusion | flops 2155872256 | bytes 17433604 | tf_op jit(solution)/shard_map/while/body/eval_jaxpr/arh,ahk->ark/dot_general | solution.py:75
  219.2 0.6 dynamic_slice.46
  220.6 9.3 %fusion.15 = f32[4,2,512,128]{2,3,0,1:T(8,128)S(1)} fusion(f32[4,2,512,128]{2,3,0,1:T(8,128)S(1)} %get-tuple-element.179, s32[]{:T(128)} %get-tuple-element.178, bf16[2,512,8192]{2,1,0:T(8,128)(2,1)} %get-tuple-element.199, f32[128]{0:T(128)S(1)} %dynamic-slice_multiply_fusion.3, f32[128]{0:T(128)S(1)} %dynamic_slice.47, f32[2,8192]{1,0:T(2,128)S(1)} %bitcast.52, ...), kind=kOutput, calls=%fused_computation.9.clone.1 | convolution fusion | flops 2155872256 | bytes 17433604 | tf_op jit(solution)/shard_map/while/body/eval_jaxpr/arh,ahk->ark/dot_general | solution.py:75
  230.1 5.9 %all_to_all.5 = f32[2,2,512,256]{2,3,1,0:T(8,128)S(1)} all-to-all(f32[2,2,512,256]{2,3,1,0:T(8,128)S(1)} %copy.22), channel_id=1, replica_groups=mesh['row_0'=4,'row_1'=4,'col'=8,'depth'=2] {'depth'}, dimensions={0} | all-to-all | bytes 4194304 | tf_op jit(solution)/shard_map/all_to_all | solution.py:33
  236.5 1.3 copy.24
  (43 shorter events, 2.8 us)
Async XLA Ops:
  6.5 180.4 %all-gather.2.cloned.1.call-start = ((), (), s32[]{:S(2)}) async-start(), calls=%async_computation.1 | async-start | bytes 18874368 | tf_op jit(solution)/shard_map/all_gather | solution.py:107
  59.3 7.0 %copy-start = (s32[512]{0:T(512)S(1)}, s32[512]{0:T(512)}, u32[]{:S(2)}) copy-start(s32[512]{0:T(512)} %param.10) | copy-start | bytes 6148
  66.4 7.1 %copy-start.1 = (f32[512]{0:T(512)S(1)}, f32[512]{0:T(512)}, u32[]{:S(2)}) copy-start(f32[512]{0:T(512)} %param.11) | copy-start | bytes 6148
  230.1 6.2 %copy-start.2 = (f32[256]{0:T(256)S(1)}, f32[256]{0:T(256)}, u32[]{:S(2)}) copy-start(f32[256]{0:T(256)} %add_sqrt_fusion) | copy-start | bytes 3076
Sparse Core Ops, SparseCore 0:
  9.1 177.7 all-gather.1
where the time goes:
time: 245 us
  waiting for transfers between devices  104 us (42%)
  blocking collectives  51.2 us (21%)
  matrix products  37.2 us (15%)
  local copies, waits for them, and re-layouts  23.7 us (10%)
  between operations  13.6 us (6%)
  other arithmetic  12.4 us (5%)
    all_gather x1, waiting for transfers between devices, body(): lax.all_gather(halves, 'col', axis=2, tiled=True)  103 us
    dot_general x4, matrix products, one(): jnp.einsum('arh,ahk->ark', piece, cauchy.astype(jnp.bfloat16), preferred_...  37.2 us
    all_gather x1, blocking collectives, in_one_piece(): out, at, done = (lax.all_gather(both, axis, axis=dim, tiled=True), 0, [])  26.9 us
    psum x2, blocking collectives, over_axes(): return functools.reduce(lax.psum, axes, shard)  18.4 us
    reduce_sum x1, other arithmetic, column_norms(): total = total + jnp.sum(cauchy * cauchy, axis=(0, 1))  9.38 us
    reshape x1, local copies, waits for them, and re-layouts, root_terms(): jnp.stack([spectrum_full[0], spectrum_full[1]], axis=1).reshape(-1)  6.99 us
    all_to_all x1, blocking collectives, summed_on_arrival(): lax.all_to_all(pieces, axis, split_axis=0, concat_axis=0, tiled=True)  5.89 us
    another operation x2, local copies, waits for them, and re-layouts, root_terms(): jnp.stack([spectrum_full[0], spectrum_full[1]], axis=1).reshape(-1)  5.07 us
  transfers between devices with their start and end apart: 1, of which 1 were waited for; matrix products, arithmetic and copies ran while one was open for 13% of the time, Pallas kernels for 0%

commit v1 on v0

--- a/solution.py
+++ b/solution.py
@@ -7,6 +7,13 @@
 from jax.sharding import PartitionSpec as P
 
 ROW = ("row_0", "row_1")
+
+
+def gather_over(shard, axis, dim):
+    peers = lax.axis_size(axis)
+    blocks = jnp.stack([shard for _ in range(peers)])
+    blocks = lax.all_to_all(blocks, axis, split_axis=0, concat_axis=0)
+    return jnp.concatenate(blocks, axis=dim)
 
 
 def over_axes(shard, axes):
@@ -104,12 +111,7 @@
     ).reshape(2, ncols * shard_width)
     share = lower_col.shape[0] // ndepth
     product, sums = panel_product(
-        lax.all_gather(halves, "col", axis=2, tiled=True),
-        seam_mine,
-        value_mine,
-        lower_col,
-        width_col,
-        fraction,
+        gather_over(halves, "col", 2), seam_mine, value_mine, lower_col, width_col, fraction
     )
     total = product
     product = summed_on_arrival(total, "depth", 2)

time: 245 us -> 516 us (2.11)
  blocking collectives: 51.2 us -> 380 us
  waiting for transfers between devices: 104 us -> 0.01 us
  local copies, waits for them, and re-layouts: 23.7 us -> 73.2 us
  between operations: 13.6 us -> 0.24 us
  starting transfers between devices: 0.01 us -> 9.13 us
    all_gather x1, blocking collectives: 26.9 us -> 356 us  [in_one_piece(): out, at, done = (lax.all_gather(both, axis, axis=dim, tiled=True), 0, [])]
    all_gather x1 -> x0, waiting for transfers between devices: 103 us -> none  [body(): lax.all_gather(halves, 'col', axis=2, tiled=True)]
    all_to_all x0 -> x1, local copies, waits for them, and re-layouts: none -> 21.8 us  [gather_over(): blocks = lax.all_to_all(blocks, axis, split_axis=0, concat_axis=0)]
    while x8 -> x9, local copies, waits for them, and re-layouts: 0.42 us -> 21.3 us  [the longest x1 20.9 us: panel_product(): products, sums = lax.map(one, jnp.arange(columns // block))]
    all_to_all x0 -> x1, starting transfers between devices: none -> 9.13 us  [gather_over(): blocks = lax.all_to_all(blocks, axis, split_axis=0, concat_axis=0)]
    another operation x0 -> x1, local copies, waits for them, and re-layouts: none -> 6.89 us  [gather_over(): blocks = jnp.stack([shard for _ in range(peers)])]
  transfers between devices with their start and end apart: 1 -> 1, of which waited for: 1 -> 0; matrix products, arithmetic and copies ran while one was open for 13% -> 6% of each run, Pallas kernels for 0% -> 0%
where the time goes in v1:
time: 516 us; the launch traced here: 514 us
  blocking collectives  380 us (74%)
  local copies, waits for them, and re-layouts  73.2 us (14%)
  matrix products  37.2 us (7%)
  other arithmetic  11.7 us (2%)
  starting transfers between devices  9.13 us (2%)
    all_gather x1, blocking collectives, in_one_piece(): out, at, done = (lax.all_gather(both, axis, axis=dim, tiled=True), 0, [])  356 us
    dot_general x4, matrix products, one(): jnp.einsum('arh,ahk->ark', piece, cauchy.astype(jnp.bfloat16), preferred_...  37.2 us
    all_to_all x1, local copies, waits for them, and re-layouts, gather_over(): blocks = lax.all_to_all(blocks, axis, split_axis=0, concat_axis=0)  21.8 us
    while x1, local copies, waits for them, and re-layouts, panel_product(): products, sums = lax.map(one, jnp.arange(columns // block))  20.9 us
    psum x2, blocking collectives, over_axes(): return functools.reduce(lax.psum, axes, shard)  18.6 us
  transfers between devices with their start and end apart: 1, of which 0 were waited for; matrix products, arithmetic and copies ran while one was open for 6% of the time, Pallas kernels for 0%

profile of v1, /device:TPU:1, one launch (start us, length us, event | category | flops | bytes accessed | tf_op | source)
XLA Modules:
  0.0 514.1 jit_solution(16635006462776944505)
XLA Ops:
  0.0 6.9 %stack.8 = bf16[8,2,512,1024]{3,2,1,0:T(8,128)(2,1)} broadcast(bf16[2,512,1024]{2,1,0:T(8,128)(2,1)} %param.8), dimensions={1,2,3} | broadcast | bytes 18874368 | tf_op jit(solution)/shard_map/stack | solution.py:14
  6.9 9.1 %all-to-all-start = ((bf16[8,2,512,1024]{3,2,1,0:T(8,128)(2,1)}), bf16[8,2,512,1024]{3,2,1,0:T(8,128)(2,1)}, u32[]{:S(2)}, u32[]{:S(2)}) async-start(bf16[8,2,512,1024]{3,2,1,0:T(8,128)(2,1)} %stack.8), calls=%async_computation | async-start | bytes 33554432 | tf_op jit(solution)/shard_map/all_to_all | solution.py:15
  16.0 0.7 fusion.7
  16.8 9.0 %psum.14 = f32[2,1024]{1,0:T(2,128)S(1)} all-reduce(f32[2,1024]{1,0:T(2,128)S(1)} %pad_maximum_fusion.2), channel_id=1, replica_groups=mesh['row_0'=4,'row_1'=4,'col'=8,'depth'=2] {'row_0'}, use_global_device_ids=true, to_apply=%region_0.1 | all-reduce | flops 2048 | bytes 16384 | tf_op jit(solution)/shard_map/psum | solution.py:20
  25.8 9.6 %psum.15 = f32[2,1024]{1,0:T(2,128)S(1)} all-reduce(f32[2,1024]{1,0:T(2,128)S(1)} %psum.14), channel_id=1, replica_groups=mesh['row_0'=4,'row_1'=4,'col'=8,'depth'=2] {'row_1'}, use_global_device_ids=true, to_apply=%region_1.2 | all-reduce | flops 2048 | bytes 16384 | tf_op jit(solution)/shard_map/psum | solution.py:20
  35.5 356.4 %all_gather.3 = f32[4,16384]{1,0:T(4,128)S(1)} all-gather(f32[4,1024]{1,0:T(4,128)S(1)} %pad_maximum_fusion.1), channel_id=1, replica_groups=mesh['row_0'=4,'row_1'=4,'col'=8,'depth'=2] {'col','depth'}, dimensions={1}, use_global_device_ids=true | all-gather | bytes 278528 | tf_op jit(solution)/shard_map/all_gather | solution.py:25
  392.1 4.9 copy.29
  397.0 6.9 %reshape.108 = f32[32768]{0:T(1024)S(1)} reshape(f32[16384,2]{1,0:T(8,128)} %copy.29) | data formatting | bytes 262144 | tf_op jit(solution)/shard_map/reshape | solution.py:45
  404.0 3.1 gather_fusion
  407.1 3.1 gather_fusion.1
  411.2 9.4 %multiply_reduce_fusion.6 = (f32[256]{0:T(256)S(1)}, f32[256]{0:T(256)S(1)}, f32[256]{0:T(256)S(1)}, f32[256]{0:T(256)S(1)}, f32[256]{0:T(256)S(1)}, /*index=5*/f32[256]{0:T(256)S(1)}, f32[256]{0:T(256)S(1)}, f32[256]{0:T(256)S(1)}) fusion(f32[2,2048]{1,0:T(2,128)S(1)} %get-tuple-element.115, f32[2,2048]{1,0:T(2,128)S(1)} %get-tuple-element.116, ...), kind=kLoop, calls=%fused_computation.17 | loop fusion | flops 41940992 | bytes 272384 | tf_op jit(solution)/shard_map/reduce_sum | solution.py:68
  420.6 0.6 add_sqrt_fusion
  421.2 21.8 %copy.30 = bf16[8,2,512,1024]{2,3,0,1:T(8,128)(2,1)} copy(bf16[8,2,512,1024]{3,2,1,0:T(8,128)(2,1)} %all-to-all-done) | data formatting | bytes 33554432 | tf_op jit(solution)/shard_map/all_to_all | solution.py:15
  443.0 20.9 %copy.31 = bf16[2,512,8192]{2,1,0:T(8,128)(2,1)} copy(bf16[2,512,8192]{1,2,0:T(8,128)(2,1)} %bitcast.50) | data formatting | bytes 33554432 | tf_op jit(solution)/shard_map/while | solution.py:87
  463.9 43.0 %while.10 = (s32[]{:T(128)}, f32[4,2,512,128]{2,3,0,1:T(8,128)S(1)}, f32[2,8,1024]{2,1,0:T(8,128)S(1)}, f32[2,8,1024]{2,1,0:T(8,128)S(1)}, s32[4]{0:T(128)S(1)},...) while((s32[]{:T(128)}, ...), condition=%wide.region_3.5_spmd, body=%wide.region_2.4_spmd.sunk | while | flops 2155872512 | bytes 17698500 | solution.py:87
  465.4 9.3 %fusion.15 = f32[4,2,512,128]{2,3,0,1:T(8,128)S(1)} fusion(f32[4,2,512,128]{2,3,0,1:T(8,128)S(1)} %get-tuple-element.197, s32[]{:T(128)} %get-tuple-element.196, bf16[2,512,8192]{2,1,0:T(8,128)(2,1)} %get-tuple-element.217, f32[128]{0:T(128)S(1)} %dynamic-slice_multiply_fusion.3, f32[128]{0:T(128)S(1)} %dynamic_slice.47, f32[2,8192]{1,0:T(2,128)S(1)} %bitcast.56, ...), kind=kOutput, calls=%fused_computation.9.clone.1 | convolution fusion | flops 2155872256 | bytes 17433604 | tf_op jit(solution)/shard_map/while/body/eval_jaxpr/arh,ahk->ark/dot_general | solution.py:82
  474.7 0.6 dynamic_slice.46
  476.1 9.3 %fusion.15 = f32[4,2,512,128]{2,3,0,1:T(8,128)S(1)} fusion(f32[4,2,512,128]{2,3,0,1:T(8,128)S(1)} %get-tuple-element.197, s32[]{:T(128)} %get-tuple-element.196, bf16[2,512,8192]{2,1,0:T(8,128)(2,1)} %get-tuple-element.217, f32[128]{0:T(128)S(1)} %dynamic-slice_multiply_fusion.3, f32[128]{0:T(128)S(1)} %dynamic_slice.47, f32[2,8192]{1,0:T(2,128)S(1)} %bitcast.56, ...), kind=kOutput, calls=%fused_computation.9.clone.1 | convolution fusion | flops 2155872256 | bytes 17433604 | tf_op jit(solution)/shard_map/while/body/eval_jaxpr/arh,ahk->ark/dot_general | solution.py:82
  485.4 0.6 dynamic_slice.46
  486.9 9.3 %fusion.15 = f32[4,2,512,128]{2,3,0,1:T(8,128)S(1)} fusion(f32[4,2,512,128]{2,3,0,1:T(8,128)S(1)} %get-tuple-element.197, s32[]{:T(128)} %get-tuple-element.196, bf16[2,512,8192]{2,1,0:T(8,128)(2,1)} %get-tuple-element.217, f32[128]{0:T(128)S(1)} %dynamic-slice_multiply_fusion.3, f32[128]{0:T(128)S(1)} %dynamic_slice.47, f32[2,8192]{1,0:T(2,128)S(1)} %bitcast.56, ...), kind=kOutput, calls=%fused_computation.9.clone.1 | convolution fusion | flops 2155872256 | bytes 17433604 | tf_op jit(solution)/shard_map/while/body/eval_jaxpr/arh,ahk->ark/dot_general | solution.py:82
  496.2 0.6 dynamic_slice.46
  497.6 9.3 %fusion.15 = f32[4,2,512,128]{2,3,0,1:T(8,128)S(1)} fusion(f32[4,2,512,128]{2,3,0,1:T(8,128)S(1)} %get-tuple-element.197, s32[]{:T(128)} %get-tuple-element.196, bf16[2,512,8192]{2,1,0:T(8,128)(2,1)} %get-tuple-element.217, f32[128]{0:T(128)S(1)} %dynamic-slice_multiply_fusion.3, f32[128]{0:T(128)S(1)} %dynamic_slice.47, f32[2,8192]{1,0:T(2,128)S(1)} %bitcast.56, ...), kind=kOutput, calls=%fused_computation.9.clone.1 | convolution fusion | flops 2155872256 | bytes 17433604 | tf_op jit(solution)/shard_map/while/body/eval_jaxpr/arh,ahk->ark/dot_general | solution.py:82
  507.1 5.2 %all_to_all.10 = f32[2,2,512,256]{2,3,1,0:T(8,128)S(1)} all-to-all(f32[2,2,512,256]{2,3,1,0:T(8,128)S(1)} %copy.33), channel_id=1, replica_groups=mesh['row_0'=4,'row_1'=4,'col'=8,'depth'=2] {'depth'}, dimensions={0} | all-to-all | bytes 4194304 | tf_op jit(solution)/shard_map/all_to_all | solution.py:40
  512.8 1.3 copy.35
  (47 shorter events, 3.4 us)
Async XLA Ops:
  6.9 28.5 %copy-start.1 = (f32[2,1024]{1,0:T(2,128)S(1)}, f32[2,1024]{1,0:T(2,128)}, u32[]{:S(2)}) copy-start(f32[2,1024]{1,0:T(2,128)} %param.9) | copy-start | bytes 24580
  6.9 414.3 %all-to-all-start = ((bf16[8,2,512,1024]{3,2,1,0:T(8,128)(2,1)}), bf16[8,2,512,1024]{3,2,1,0:T(8,128)(2,1)}, u32[]{:S(2)}, u32[]{:S(2)}) async-start(bf16[8,2,512,1024]{3,2,1,0:T(8,128)(2,1)} %stack.8), calls=%async_computation | async-start | bytes 33554432 | tf_op jit(solution)/shard_map/all_to_all | solution.py:15
  397.0 6.9 %copy-start = (s32[512]{0:T(512)S(1)}, s32[512]{0:T(512)}, u32[]{:S(2)}) copy-start(s32[512]{0:T(512)} %param.10) | copy-start | bytes 6148
  403.9 7.1 %copy-start.2 = (f32[512]{0:T(512)S(1)}, f32[512]{0:T(512)}, u32[]{:S(2)}) copy-start(f32[512]{0:T(512)} %param.11) | copy-start | bytes 6148
  507.1 5.5 %copy-start.3 = (f32[256]{0:T(256)S(1)}, f32[256]{0:T(256)}, u32[]{:S(2)}) copy-start(f32[256]{0:T(256)} %add_sqrt_fusion) | copy-start | bytes 3076
